TPU v7x, 32 devices: a whole 2x2x4 slice. The times are simulated.
32 devices in a mesh: section: 2 (over core), dp: 2 (over y), tensor: 8 (over z, x).
Axes of the slice: x: 2, y: 2, z: 4, core: 2. Of those that a mesh axis runs over, the one named last changes fastest.
Arguments:
- residual_parts: bfloat16 [2, 768, 16384], P('section', 'dp', 'tensor'), may hold values from -120 to 120
- attn_out: bfloat16 [2, 768, 16384], P('section', 'dp', 'tensor'), may hold values from -6 to 6
- ffn_input: bfloat16 [2, 768, 53248], P('section', 'dp', 'tensor'), may hold values from -6 to 6
- norm_gain: float32 [2, 16384], P('section', 'tensor'), may hold values from 0.25 to 1.75
- mixing: bfloat16 [2, 52, 52], P('section'), may hold values from -0.875 to 0.875
- blocks: int32 [2, 2], P('section'), may hold values from 0 to 25, as said below
Outputs:
- hess_in: float32 [2, 16384, 1024], P('section', 'tensor', 'dp')
- hess_o: float32 [2, 16384, 1024], P('section', 'tensor', 'dp')
- hess_down: float32 [2, 2048, 2048], P('section', 'tensor', 'dp')
Inputs may be any that keep to these rules, and one draw needn't show every extreme that they name: `blocks`: entry [s, 0] is below 16; entry [s, 1] is below 26. In every draw one layer has entry [s, 0] = 0 and entry [s, 1] = 25.
All inputs are finite; a program needn't handle non-finite values.
Results may differ from a plain program's by a relative error of at most 0.0038.
Values may be sent and summed in bfloat16 or wider, within the bound.
A program may use at most 128 MiB of HBM per device.

v0:
```python
import math
import jax
import jax.numpy as jnp
from jax import lax
from jax.sharding import PartitionSpec as P

D = 16384
KB = 52
HBLK = 1024
BLK = 2048
EPS = 1e-05


def passed_along(x, axis, by):
    devices = lax.axis_size(axis)
    pairs = [(i, i + by) for i in range(devices) if 0 <= i + by < devices]
    return lax.ppermute(x, axis, pairs)


def broadcast(value, axis, source):
    kept = jnp.where(lax.axis_index(axis) == source, value, 0).astype(value.dtype)
    return lax.psum(kept, axis)


def bit_parity(values):
    total = jnp.zeros_like(values)
    for position in range(16):
        total = total + values // (1 << position) % 2
    return total % 2


def sylvester(order):
    index = jnp.arange(order, dtype=jnp.int32)
    parity = bit_parity(jnp.bitwise_and(index[:, None], index[None, :]))
    return (1 - 2 * parity).astype(jnp.float32)


def gram(left, right):
    return lax.dot_general(
        left, right, (((0,), (0,)), ((), ())), preferred_element_type=jnp.float32
    )


def local(residual_parts, attn_out, ffn_input, norm_gain, mixing, blocks):
    local_d = residual_parts.shape[2]
    local_f = ffn_input.shape[2]
    token_rows = residual_parts.shape[1]
    own_part = residual_parts[0]
    earlier = passed_along(own_part, "section", 1)
    layer_in = earlier.astype(jnp.float32) + own_part.astype(jnp.float32)
    square_total = lax.psum(jnp.sum(layer_in * layer_in, axis=1), "tensor")
    normed = (layer_in * lax.rsqrt(square_total / D + EPS)[:, None] * norm_gain[0][None, :]).astype(
        jnp.bfloat16
    )
    attention = attn_out[0]
    first_col = blocks[0, 0] * HBLK
    width = min(HBLK, local_d)
    offset = first_col % local_d
    norm_slab = lax.dynamic_slice_in_dim(normed, offset, width, 1)
    attn_slab = lax.dynamic_slice_in_dim(attention, offset, width, 1)
    norm_list, attn_list = ([], [])
    owner = first_col // local_d + 0
    norm_got = broadcast(norm_slab, "tensor", owner)
    attn_got = broadcast(attn_slab, "tensor", owner)
    norm_list.append(norm_got)
    attn_list.append(attn_got)
    norm_block = norm_list[0]
    attn_block = attn_list[0]
    tensor_count = lax.axis_size("tensor")
    member = lax.axis_index("tensor")
    a_local = local_f // KB
    order_a = a_local * tensor_count
    cube = ffn_input[0].reshape(token_rows, a_local, KB)
    mixed = jnp.einsum("rak,kc->rac", cube, mixing[0], preferred_element_type=jnp.float32)
    turned = jnp.einsum("rac,ae->rec", mixed, sylvester(a_local), precision=lax.Precision.HIGHEST)
    turned = turned.reshape(token_rows, local_f)
    start = blocks[0, 1] * BLK
    doubled = jnp.concatenate([turned, turned], axis=1)
    window = lax.dynamic_slice_in_dim(doubled, start % local_f, BLK, 1)
    target = (start + jnp.arange(BLK, dtype=jnp.int32)) // local_f
    parity = bit_parity(jnp.bitwise_and(target, member))
    signs = (1 - 2 * parity).astype(jnp.float32) / math.sqrt(order_a)
    term = window * signs[None, :]
    share = BLK // tensor_count
    rotated = lax.psum(term, "tensor").astype(jnp.bfloat16)
    own_cols = lax.dynamic_slice_in_dim(rotated, member * share, share, 1)
    part_in = gram(normed, norm_block)
    part_o = gram(attention, attn_block)
    part_down = gram(own_cols, rotated)
    summed = (
        lax.psum_scatter(part_in, "dp", scatter_dimension=1, tiled=True),
        lax.psum_scatter(part_o, "dp", scatter_dimension=1, tiled=True),
        lax.psum_scatter(part_down, "dp", scatter_dimension=1, tiled=True),
    )
    scale = 2.0 / (token_rows * lax.axis_size("dp"))
    hess_in = (scale * summed[0])[None]
    hess_o = (scale * summed[1])[None]
    hess_down = (scale * summed[2])[None]
    return (hess_in, hess_o, hess_down)


def solution(mesh):
    return jax.shard_map(
        local,
        mesh=mesh,
        in_specs=(
            P("section", "dp", "tensor"),
            P("section", "dp", "tensor"),
            P("section", "dp", "tensor"),
            P("section", "tensor"),
            P("section", None, None),
            P("section", None),
        ),
        out_specs=(
            P("section", "tensor", "dp"),
            P("section", "tensor", "dp"),
            P("section", "tensor", "dp"),
        ),
        check_vma=False,
    )
```

profile of v0, /device:TPU:0, one launch (start us, length us, event | category | flops | bytes accessed | tf_op | source)
XLA Modules:
  0.0 523.9 jit_solution(5240815388376950331)
XLA Ops:
  8.0 0.0 copy-start
  8.0 0.0 all-reduce.5.cloned.1.call-start
  8.1 3.6 collective-permute-start
  11.7 7.8 %copy.11 = bf16[1,384,6656]{1,2,0:T(8,128)(2,1)} copy(bf16[1,384,6656]{2,1,0:T(8,128)(2,1)} %param.8) | data formatting | bytes 10223616 | tf_op args[2]
  19.4 8.1 %reshape_squeeze.3 = bf16[384,128,52]{0,2,1:T(8,128)(2,1)} reshape(bf16[1,384,6656]{1,2,0:T(8,128)(2,1)} %copy.11) | data formatting | bytes 10223616 | tf_op jit(solution)/shard_map/reshape;squeeze | solution.py:73
  27.5 0.0 copy-done
  27.5 0.0 copy-start.5
  27.5 8.4 %fusion.156 = f32[384,128,52]{0,2,1:T(8,128)} fusion(bf16[384,128,52]{0,2,1:T(8,128)(2,1)} %reshape_squeeze.3, bf16[1,52,52]{2,1,0:T(8,128)(2,1)S(1)} %copy-done), kind=kOutput, calls=%fused_computation.259 | convolution fusion | flops 265814016 | bytes 15340832 | tf_op jit(solution)/shard_map/rak,kc->rac/dot_general | solution.py:74
  35.9 0.0 copy-done.5
  35.9 0.6 fusion.253
  37.8 15.9 %fusion.2 = f32[384,128,52]{0,1,2:T(8,128)S(1)} fusion(f32[384,128,52]{0,2,1:T(8,128)} %fusion.156), kind=kOutput, calls=%fused_computation.7 | convolution fusion | flops 3931668480 | bytes 20447232 | tf_op jit(solution)/shard_map/rac,ae->rec/dot_general | solution.py:75
  53.7 10.1 %copy.12 = f32[384,128,52]{0,2,1:T(8,128)} copy(f32[384,128,52]{0,1,2:T(8,128)S(1)} %fusion.2) | data formatting | bytes 20447232 | tf_op jit(solution)/shard_map/rac,ae->rec/transpose | solution.py:75
  63.8 11.5 %reshape.392 = f32[384,6656]{0,1:T(8,128)} reshape(f32[384,128,52]{0,2,1:T(8,128)} %copy.12) | data formatting | bytes 20447232 | tf_op jit(solution)/shard_map/reshape | solution.py:76
  75.4 0.1 fusion.207
  75.5 2.9 fusion.6
  78.4 2.5 select_bitcast_fusion
  80.8 0.0 copy-start.4
  80.8 0.0 collective-permute-done
  80.8 2.5 multiply_reduce_fusion
  83.3 129.9 %all-reduce.6 = (f32[384]{0:T(512)S(1)}, bf16[384,2048]{0,1:T(8,128)(2,1)}) all-reduce(f32[384]{0:T(512)S(1)} %multiply_reduce_fusion, f32[384,2048]{0,1:T(8,128)S(1)} %fusion.6), channel_id=1, replica_groups=mesh['section'=2,'dp'=2,'tensor'=8] {'tensor'}, use_global_device_ids=true, to_apply=%region_1.0 | all-reduce | flops 786816 | bytes 4721664 | tf_op jit(solution)/shard_map/psum | solution.py:51
  213.2 0.0 copy-done.4
  213.2 2.6 multiply_convert_fusion
  215.8 1.3 dynamic-slice_select_fusion
  217.1 0.0 all-reduce.5.cloned.1.call-update
  217.1 0.0 copy-start.2
  217.2 0.0 reduce-scatter.8.cloned.1.call-start
  217.2 3.7 fusion.8
  220.9 0.0 reduce-scatter.8.cloned.1.call-update
  220.9 0.3 reduce-scatter.6.cloned.1.call-start
  221.2 83.6 %all-reduce.5.cloned.1.call-done = (bf16[384,1024]{1,0:T(8,128)(2,1)}, bf16[384,1024]{1,0:T(8,128)(2,1)}) async-done(((bf16[384,1024]{1,0:T(8,128)(2,1)}, bf16[384,1024]{1,0:T(8,128)(2,1)}), (bf16[384,1024]{1,0:T(8,128)(2,1)}, bf16[384,1024]{1,0:T(8,128)(2,1)})) %all-reduce.5.cloned.1.call-update) | async-done | bytes 1572880 | tf_op jit(solution)/shard_map/psum | solution.py:22
  304.7 0.0 copy-done.2
  304.8 6.7 %convolution_bitcast_fusion = f32[2048,1024]{1,0:T(8,128)} fusion(bf16[384,1024]{1,0:T(8,128)(2,1)} %get-tuple-element.6, bf16[1,384,2048]{2,1,0:T(8,128)(2,1)S(1)} %copy-done.2), kind=kOutput, calls=%fused_computation.4 | convolution fusion | flops 1610612736 | bytes 10747904 | tf_op jit(solution)/shard_map/dot_general | solution.py:39
  311.5 0.0 copy-start.3
  311.5 0.0 reduce-scatter.6.cloned.1.call-update
  311.5 0.0 reduce-scatter.4.cloned.1.call-start
  311.6 1.1 copy-done.3
  312.6 5.9 %fusion.254 = f32[2048,1024]{1,0:T(8,128)} fusion(bf16[384,2048]{1,0:T(8,128)(2,1)S(1)} %multiply_convert_fusion, bf16[384,1024]{1,0:T(8,128)(2,1)S(1)} %copy-done.3), kind=kOutput, calls=%fused_computation.458 | convolution fusion | flops 1610612736 | bytes 10747904 | tf_op jit(solution)/shard_map/dot_general | solution.py:39
  318.5 0.0 reduce-scatter.4.cloned.1.call-update
  318.5 0.0 reduce-scatter.8.cloned.1.call-done
  318.6 2.3 multiply_bitcast_fusion.2
  320.9 89.2 %reduce-scatter.6.cloned.1.call-done = f32[2048,512]{1,0:T(8,128)} async-done(((f32[2048,1024]{1,0:T(8,128)}), f32[2048,512]{1,0:T(8,128)}) %reduce-scatter.6.cloned.1.call-update) | async-done | bytes 4194320 | tf_op jit(solution)/shard_map/reduce_scatter | solution.py:92
  410.1 0.0 copy-start.1
  410.1 4.7 multiply_bitcast_fusion
  414.8 96.7 %reduce-scatter.4.cloned.1.call-done = f32[2048,512]{1,0:T(8,128)} async-done(((f32[2048,1024]{1,0:T(8,128)}), f32[2048,512]{1,0:T(8,128)}) %reduce-scatter.4.cloned.1.call-update) | async-done | bytes 4194320 | tf_op jit(solution)/shard_map/reduce_scatter | solution.py:91
  511.6 4.7 multiply_bitcast_fusion.1
  516.3 0.0 copy-done.1
  (1 shorter events, 0.0 us)
Async XLA Ops:
  8.0 19.5 %copy-start = (bf16[1,52,52]{2,1,0:T(8,128)(2,1)S(1)}, bf16[1,52,52]{2,1,0:T(8,128)(2,1)}, u32[]{:S(2)}) copy-start(bf16[1,52,52]{2,1,0:T(8,128)(2,1)} %param.10) | copy-start | bytes 16228
  8.0 296.7 %all-reduce.5.cloned.1.call-start = ((), (), s32[]{:S(2)}) async-start(), calls=%async_computation.6 | async-start | bytes 3145728 | tf_op jit(solution)/shard_map/psum | solution.py:22
  8.1 72.8 %collective-permute-start = (bf16[384,2048]{1,0:T(8,128)(2,1)}, bf16[384,2048]{1,0:T(8,128)(2,1)}, u32[]{:S(2)}, u32[]{:S(2)}) collective-permute-start(bf16[384,2048]{1,0:T(8,128)(2,1)} %bitcast.37), channel_id=1, source_target_pairs={{0,16},{1,17},{2,18},{3,19},{4,20},{5,21},{6,22},{7,23},{8,24},{9,... | collective-permute-start | bytes 4718600 | tf_op jit(solution)/shard_map/ppermute | solution.py:17
  27.5 8.4 %copy-start.5 = (s32[1,2]{1,0:T(1,128)S(1)}, s32[1,2]{1,0:T(1,128)}, u32[]{:S(2)}) copy-start(s32[1,2]{1,0:T(1,128)} %param.11) | copy-start | bytes 28
  80.8 132.4 %copy-start.4 = (f32[1,2048]{1,0:T(1,128)S(1)}, f32[1,2048]{1,0:T(1,128)}, u32[]{:S(2)}) copy-start(f32[1,2048]{1,0:T(1,128)} %param.9) | copy-start | bytes 24580
  217.1 87.6 %copy-start.2 = (bf16[1,384,2048]{2,1,0:T(8,128)(2,1)S(1)}, bf16[1,384,2048]{2,1,0:T(8,128)(2,1)}, u32[]{:S(2)}) copy-start(bf16[1,384,2048]{2,1,0:T(8,128)(2,1)} %param.7) | copy-start | bytes 4718596
  217.2 101.4 %reduce-scatter.8.cloned.1.call-start = ((), (), s32[]{:S(2)}) async-start(), calls=%async_computation.5 | async-start | bytes 3145728 | tf_op jit(solution)/shard_map/reduce_scatter | solution.py:93
  220.9 189.2 %reduce-scatter.6.cloned.1.call-start = ((), (), s32[]{:S(2)}) async-start(), calls=%async_computation.4 | async-start | bytes 12582912 | tf_op jit(solution)/shard_map/reduce_scatter | solution.py:92
  311.5 1.1 copy-start.3
  311.5 200.0 %reduce-scatter.4.cloned.1.call-start = ((), (), s32[]{:S(2)}) async-start(), calls=%async_computation.3 | async-start | bytes 12582912 | tf_op jit(solution)/shard_map/reduce_scatter | solution.py:91
  410.1 106.2 %copy-start.1 = (bf16[1,52,52]{2,1,0:T(8,128)(2,1)S(1)}, bf16[1,52,52]{2,1,0:T(8,128)(2,1)}, u32[]{:S(2)}) copy-start(bf16[1,52,52]{2,1,0:T(8,128)(2,1)} %param.10) | copy-start | bytes 16228
Sparse Core Ops, SparseCore 0:
  217.3 87.4 all-reduce.4
Sparse Core Ops, SparseCore 1:
  221.0 29.9 reduce-scatter.7
  311.6 98.4 reduce-scatter.5
  412.3 99.2 reduce-scatter.3
where the time goes:
time: 525 us; the launch traced here: 524 us
  waiting for transfers between devices  270 us (51%)
  blocking collectives  130 us (25%)
  matrix products  40.5 us (8%)
  local copies, waits for them, and re-layouts  39.2 us (7%)
  other arithmetic  23.6 us (4%)
  between operations  17.1 us (3%)
    psum x1, blocking collectives, local(): square_total = lax.psum(jnp.sum(layer_in * layer_in, axis=1), 'tensor')  130 us
    reduce_scatter x1, waiting for transfers between devices, local(): lax.psum_scatter(part_in, 'dp', scatter_dimension=1, tiled=True)  96.7 us
    reduce_scatter x1, waiting for transfers between devices, local(): lax.psum_scatter(part_o, 'dp', scatter_dimension=1, tiled=True)  89.2 us
    psum x1, waiting for transfers between devices, broadcast(): return lax.psum(kept, axis)  83.6 us
    dot_general x3, matrix products, gram(): lax.dot_general(left, right, (((0,), (0,)), ((), ())), preferred_element_...  16.3 us
    dot_general x1, matrix products, local(): jnp.einsum('rac,ae->rec', mixed, sylvester(a_local), precision=lax.Precis...  15.9 us
    reshape x1, local copies, waits for them, and re-layouts, local(): turned = turned.reshape(token_rows, local_f)  11.5 us
  transfers between devices with their start and end apart: 5, of which 3 were waited for; matrix products, arithmetic and copies ran while one was open for 17% of the time, Pallas kernels for 0%

commit v1 on v0

--- a/solution.py
+++ b/solution.py
@@ -19,7 +19,7 @@
 
 def broadcast(value, axis, source):
     kept = jnp.where(lax.axis_index(axis) == source, value, 0).astype(value.dtype)
-    return lax.psum(kept, axis)
+    return jnp.sum(lax.all_gather(kept, axis), axis=0)
 
 
 def bit_parity(values):

time: 525 us -> 473 us (0.901)
  waiting for transfers between devices: 270 us -> 206 us
  other arithmetic: 23.6 us -> 32 us
    psum x1 -> x0, waiting for transfers between devices: 83.6 us -> none  [broadcast(): return lax.psum(kept, axis)]
    all_gather x0 -> x2, waiting for transfers between devices: none -> 83.4 us  [broadcast(): return jnp.sum(lax.all_gather(kept, axis), axis=0)]
    reduce_scatter x1, waiting for transfers between devices: 89.2 us -> 25.4 us  [local(): lax.psum_scatter(part_o, 'dp', scatter_dimension=1, tiled=True)]
    reduce_sum x0 -> x2, other arithmetic: none -> 8.61 us  [broadcast(): return jnp.sum(lax.all_gather(kept, axis), axis=0)]
  transfers between devices with their start and end apart: 5 -> 6, of which waited for: 3 -> 3; matrix products, arithmetic and copies ran while one was open for 17% -> 22% of each run, Pallas kernels for 0% -> 0%
where the time goes in v1:
time: 473 us; the launch traced here: 472 us
  waiting for transfers between devices  206 us (44%)
  blocking collectives  135 us (29%)
  matrix products  39.3 us (8%)
  local copies, waits for them, and re-layouts  38.9 us (8%)
  other arithmetic  32 us (7%)
  between operations  17.1 us (4%)
    psum x1, blocking collectives, local(): square_total = lax.psum(jnp.sum(layer_in * layer_in, axis=1), 'tensor')  135 us
    reduce_scatter x1, waiting for transfers between devices, local(): lax.psum_scatter(part_in, 'dp', scatter_dimension=1, tiled=True)  96.7 us
    all_gather x2, waiting for transfers between devices, broadcast(): return jnp.sum(lax.all_gather(kept, axis), axis=0)  83.4 us
    reduce_scatter x1, waiting for transfers between devices, local(): lax.psum_scatter(part_o, 'dp', scatter_dimension=1, tiled=True)  25.4 us
    dot_general x1, matrix products, local(): jnp.einsum('rac,ae->rec', mixed, sylvester(a_local), precision=lax.Precis...  15.9 us
    dot_general x3, matrix products, gram(): lax.dot_general(left, right, (((0,), (0,)), ((), ())), preferred_element_...  15 us
    reshape x1, local copies, waits for them, and re-layouts, local(): turned = turned.reshape(token_rows, local_f)  11.6 us
    transpose x1, local copies, waits for them, and re-layouts, local(): jnp.einsum('rac,ae->rec', mixed, sylvester(a_local), precision=lax.Precis...  10.1 us
  transfers between devices with their start and end apart: 6, of which 3 were waited for; matrix products, arithmetic and copies ran while one was open for 22% of the time, Pallas kernels for 0%

profile of v1, /device:TPU:0, one launch (start us, length us, event | category | flops | bytes accessed | tf_op | source)
XLA Modules:
  0.0 471.6 jit_solution(5819857293900433226)
XLA Ops:
  8.0 0.0 copy-start
  8.0 0.0 all-gather.4.cloned.1.call-start
  8.1 1.3 fusion.253
  10.1 2.4 dynamic-slice_select_fusion
  12.5 0.0 all-gather.4.cloned.1.call-update
  12.5 0.0 all-gather.6.cloned.1.call-start
  12.6 3.5 collective-permute-start
  16.1 7.8 %copy.14 = bf16[1,384,6656]{1,2,0:T(8,128)(2,1)} copy(bf16[1,384,6656]{2,1,0:T(8,128)(2,1)} %param.8) | data formatting | bytes 10223616 | tf_op args[2]
  23.9 8.1 %reshape_squeeze.3 = bf16[384,128,52]{0,2,1:T(8,128)(2,1)} reshape(bf16[1,384,6656]{1,2,0:T(8,128)(2,1)} %copy.14) | data formatting | bytes 10223616 | tf_op jit(solution)/shard_map/reshape;squeeze | solution.py:73
  32.0 0.0 copy-done
  32.0 8.4 %fusion.156 = f32[384,128,52]{0,2,1:T(8,128)} fusion(bf16[384,128,52]{0,2,1:T(8,128)(2,1)} %reshape_squeeze.3, bf16[1,52,52]{2,1,0:T(8,128)(2,1)S(1)} %copy-done), kind=kOutput, calls=%fused_computation.259 | convolution fusion | flops 265814016 | bytes 15340832 | tf_op jit(solution)/shard_map/rak,kc->rac/dot_general | solution.py:74
  41.0 15.9 %fusion.2 = f32[384,128,52]{0,1,2:T(8,128)S(1)} fusion(f32[384,128,52]{0,2,1:T(8,128)} %fusion.156), kind=kOutput, calls=%fused_computation.7 | convolution fusion | flops 3931668480 | bytes 20447232 | tf_op jit(solution)/shard_map/rac,ae->rec/dot_general | solution.py:75
  56.9 10.1 %copy.17 = f32[384,128,52]{0,2,1:T(8,128)} copy(f32[384,128,52]{0,1,2:T(8,128)S(1)} %fusion.2) | data formatting | bytes 20447232 | tf_op jit(solution)/shard_map/rac,ae->rec/transpose | solution.py:75
  67.1 11.6 %reshape.389 = f32[384,6656]{0,1:T(8,128)} reshape(f32[384,128,52]{0,2,1:T(8,128)} %copy.17) | data formatting | bytes 20447232 | tf_op jit(solution)/shard_map/reshape | solution.py:76
  78.6 0.1 fusion.207
  78.8 0.0 copy-start.2
  78.8 3.0 fusion.6
  81.7 0.0 copy-start.4
  81.8 0.0 collective-permute-done
  81.8 0.0 copy-done.2
  81.8 2.0 multiply_reduce_fusion
  83.8 134.7 %all-reduce.2 = (f32[384]{0:T(512)S(1)}, bf16[384,2048]{0,1:T(8,128)(2,1)}) all-reduce(f32[384]{0:T(512)S(1)} %multiply_reduce_fusion, f32[384,2048]{0,1:T(8,128)S(1)} %fusion.6), channel_id=1, replica_groups=mesh['section'=2,'dp'=2,'tensor'=8] {'tensor'}, use_global_device_ids=true, to_apply=%region_1.0 | all-reduce | flops 786816 | bytes 4721664 | tf_op jit(solution)/shard_map/psum | solution.py:51
  218.5 0.0 copy-done.4
  218.5 0.0 copy-start.3
  218.5 2.7 multiply_convert_fusion
  221.2 1.3 dynamic-slice_select_fusion.1
  222.5 0.0 all-gather.6.cloned.1.call-update
  222.5 0.0 reduce-scatter.8.cloned.1.call-start
  222.6 0.0 copy-done.3
  222.6 2.1 fusion.8
  224.6 0.0 reduce-scatter.8.cloned.1.call-update
  224.7 0.3 reduce-scatter.6.cloned.1.call-start
  224.9 0.0 all-gather.4.cloned.1.call-done
  225.0 4.3 reduce_sum.35
  229.3 7.4 %convolution_bitcast_fusion = f32[2048,1024]{1,0:T(8,128)} fusion(bf16[384,1024]{1,0:T(8,128)(2,1)S(1)} %reduce_sum.35, bf16[1,384,2048]{2,1,0:T(8,128)(2,1)} %param.7), kind=kOutput, calls=%fused_computation.4 | convolution fusion | flops 1610612736 | bytes 10747904 | tf_op jit(solution)/shard_map/dot_general | solution.py:39
  236.7 0.0 reduce-scatter.6.cloned.1.call-update
  236.7 0.0 reduce-scatter.4.cloned.1.call-start
  236.7 83.3 %all-gather.6.cloned.1.call-done = bf16[3072,1024]{1,0:T(8,128)(2,1)} async-done(((bf16[384,1024]{1,0:T(8,128)(2,1)}), bf16[3072,1024]{1,0:T(8,128)(2,1)}) %all-gather.6.cloned.1.call-update) | async-done | bytes 6291472 | tf_op jit(solution)/shard_map/all_gather | solution.py:22
  320.1 4.3 reduce_sum.34
  324.4 5.6 %fusion.254 = f32[2048,1024]{1,0:T(8,128)} fusion(bf16[384,2048]{1,0:T(8,128)(2,1)S(1)} %multiply_convert_fusion, bf16[384,1024]{1,0:T(8,128)(2,1)S(1)} %reduce_sum.34), kind=kOutput, calls=%fused_computation.458 | convolution fusion | flops 1610612736 | bytes 10747904 | tf_op jit(solution)/shard_map/dot_general | solution.py:39
  330.0 0.0 reduce-scatter.4.cloned.1.call-update
  330.0 0.0 reduce-scatter.8.cloned.1.call-done
  330.0 2.4 multiply_bitcast_fusion.2
  332.4 25.4 %reduce-scatter.6.cloned.1.call-done = f32[2048,512]{1,0:T(8,128)} async-done(((f32[2048,1024]{1,0:T(8,128)}), f32[2048,512]{1,0:T(8,128)}) %reduce-scatter.6.cloned.1.call-update) | async-done | bytes 4194320 | tf_op jit(solution)/shard_map/reduce_scatter | solution.py:92
  357.8 4.7 %multiply_bitcast_fusion = f32[1,2048,512]{2,1,0:T(8,128)} fusion(f32[2048,512]{1,0:T(8,128)} %reduce-scatter.6.cloned.1.call-done), kind=kLoop, calls=%fused_computation.5 | loop fusion | flops 1048576 | bytes 8388608 | tf_op jit(solution)/shard_map/broadcast_in_dim | solution.py:97
  362.6 96.7 %reduce-scatter.4.cloned.1.call-done = f32[2048,512]{1,0:T(8,128)} async-done(((f32[2048,1024]{1,0:T(8,128)}), f32[2048,512]{1,0:T(8,128)}) %reduce-scatter.4.cloned.1.call-update) | async-done | bytes 4194320 | tf_op jit(solution)/shard_map/reduce_scatter | solution.py:91
  459.3 4.7 multiply_bitcast_fusion.1
  464.0 0.0 copy-done.1
  (2 shorter events, 0.0 us)
Async XLA Ops:
  8.0 24.0 %copy-start = (bf16[1,52,52]{2,1,0:T(8,128)(2,1)S(1)}, bf16[1,52,52]{2,1,0:T(8,128)(2,1)}, u32[]{:S(2)}) copy-start(bf16[1,52,52]{2,1,0:T(8,128)(2,1)} %param.10) | copy-start | bytes 16228
  8.0 217.0 %all-gather.4.cloned.1.call-start = ((), (), s32[]{:S(2)}) async-start(), calls=%async_computation.4 | async-start | bytes 7077888 | tf_op jit(solution)/shard_map/all_gather | solution.py:22
  12.5 307.5 %all-gather.6.cloned.1.call-start = ((), (), s32[]{:S(2)}) async-start(), calls=%async_computation.7 | async-start | bytes 7077888 | tf_op jit(solution)/shard_map/all_gather | solution.py:22
  12.6 69.2 %collective-permute-start = (bf16[384,2048]{1,0:T(8,128)(2,1)}, bf16[384,2048]{1,0:T(8,128)(2,1)}, u32[]{:S(2)}, u32[]{:S(2)}) collective-permute-start(bf16[384,2048]{1,0:T(8,128)(2,1)} %bitcast.38), channel_id=1, source_target_pairs={{0,16},{1,17},{2,18},{3,19},{4,20},{5,21},{6,22},{7,23},{8,24},{9,... | collective-permute-start | bytes 4718600 | tf_op jit(solution)/shard_map/ppermute | solution.py:17
  78.8 3.0 copy-start.2
  81.7 136.7 %copy-start.4 = (f32[1,2048]{1,0:T(1,128)S(1)}, f32[1,2048]{1,0:T(1,128)}, u32[]{:S(2)}) copy-start(f32[1,2048]{1,0:T(1,128)} %param.9) | copy-start | bytes 24580
  218.5 4.1 copy-start.3
  222.5 107.5 %reduce-scatter.8.cloned.1.call-start = ((), (), s32[]{:S(2)}) async-start(), calls=%async_computation.6 | async-start | bytes 3145728 | tf_op jit(solution)/shard_map/reduce_scatter | solution.py:93
  224.7 133.2 %reduce-scatter.6.cloned.1.call-start = ((), (), s32[]{:S(2)}) async-start(), calls=%async_computation.5 | async-start | bytes 12582912 | tf_op jit(solution)/shard_map/reduce_scatter | solution.py:92
  236.7 222.6 %reduce-scatter.4.cloned.1.call-start = ((), (), s32[]{:S(2)}) async-start(), calls=%async_computation.3 | async-start | bytes 12582912 | tf_op jit(solution)/shard_map/reduce_scatter | solution.py:91
  357.8 106.2 %copy-start.1 = (bf16[1,52,52]{2,1,0:T(8,128)(2,1)S(1)}, bf16[1,52,52]{2,1,0:T(8,128)(2,1)}, u32[]{:S(2)}) copy-start(bf16[1,52,52]{2,1,0:T(8,128)(2,1)} %param.10) | copy-start | bytes 16228
Sparse Core Ops, SparseCore 0:
  12.7 122.4 all-gather.3
  222.6 97.3 all-gather.5
Sparse Core Ops, SparseCore 1:
  225.8 30.5 reduce-scatter.7
  258.5 99.2 reduce-scatter.5
  360.0 99.2 reduce-scatter.3
